TPU v7x, 32 devices: a whole 2x2x4 slice. The times are simulated.
32 devices in a mesh: depth: 4 (over z), row: 2 (over x), col: 4 (over y, core).
Axes of the slice: x: 2, y: 2, z: 4, core: 2. Of those that a mesh axis runs over, the one named last changes fastest.
Arguments:
- tokens: bfloat16 [192, 8192], P('row', ('depth', 'col')), may hold values from -6 to 6
- cotangent: bfloat16 [192, 8192], P('row', ('depth', 'col')), may hold values from -1.609375 to 1.609375
- gate_weight: bfloat16 [8192, 14336], P(('depth', 'col'), 'row'), may hold values from -0.0625 to 0.0625
- up_weight: bfloat16 [8192, 14336], P(('depth', 'col'), 'row'), may hold values from -0.0625 to 0.0625
- down_weight: bfloat16 [14336, 8192], P('row', ('depth', 'col')), may hold values from -0.046875 to 0.046875
Outputs:
- input_grad: bfloat16 [192, 8192], P('row', ('depth', 'col'))
- gate_grad: bfloat16 [8192, 14336], P(('depth', 'col'), 'row')
- up_grad: bfloat16 [8192, 14336], P(('depth', 'col'), 'row')
- down_grad: bfloat16 [14336, 8192], P('row', ('depth', 'col'))
All inputs are finite; a program needn't handle non-finite values.
Results may differ from a plain program's by a relative error of at most 0.0065.
Values may be sent and summed in bfloat16 or wider, within the bound.
No kernel may reach another device: no remote copies, remote signals or barrier semaphores. Data moves between devices by JAX's collectives and lax.ppermute only.
A program may use at most 128 MiB of HBM per device.

v0:
```python
import jax
import jax.numpy as jnp
from jax import lax
from jax.sharding import PartitionSpec as P


def swiglu_back(gate, up, back):
    sig = jax.nn.sigmoid(gate)
    hidden = (gate * sig * up).astype(jnp.bfloat16)
    grad_gate = (back * up * sig * (1.0 + gate * (1.0 - sig))).astype(jnp.bfloat16)
    grad_up = (back * gate * sig).astype(jnp.bfloat16)
    return (hidden, grad_gate, grad_up)


def contract_rows(left, right):
    return lax.dot_general(
        left, right, (((0,), (0,)), ((), ())), preferred_element_type=jnp.float32
    )


def contract_cols(left, right):
    return lax.dot_general(
        left, right, (((1,), (1,)), ((), ())), preferred_element_type=jnp.float32
    )


def stationary(tokens, cotangent, gate_weight, up_weight, down_weight):
    rows_all, cot_all = (
        lax.all_gather(tokens, "row", axis=0, tiled=True),
        lax.all_gather(cotangent, "row", axis=0, tiled=True),
    )
    width = gate_weight.shape[1]
    rows_part = rows_all
    cot_part = cot_all
    gate_part = jnp.dot(rows_part, gate_weight, preferred_element_type=jnp.float32)
    up_part = jnp.dot(rows_part, up_weight, preferred_element_type=jnp.float32)
    back_part = contract_cols(cot_part, down_weight)
    summed = lax.psum_scatter(
        jnp.concatenate([gate_part, up_part, back_part], axis=1),
        ("depth", "col"),
        scatter_dimension=0,
        tiled=True,
    )
    hidden, grad_gate, grad_up = swiglu_back(
        summed[:, :width], summed[:, width : 2 * width], summed[:, 2 * width :]
    )
    hidden_piece = lax.all_gather(hidden, ("depth", "col"), axis=0, tiled=True)
    gate_piece = lax.all_gather(grad_gate, ("depth", "col"), axis=0, tiled=True)
    up_piece = lax.all_gather(grad_up, ("depth", "col"), axis=0, tiled=True)
    rows_part = rows_all
    cot_part = cot_all
    acc_gate = contract_rows(rows_part, gate_piece)
    acc_up = contract_rows(rows_part, up_piece)
    acc_down = contract_rows(hidden_piece, cot_part)
    block = contract_cols(gate_piece, gate_weight) + contract_cols(up_piece, up_weight)
    input_grad = lax.psum_scatter(block, "row", scatter_dimension=0, tiled=True).astype(
        jnp.bfloat16
    )
    return (
        input_grad,
        acc_gate.astype(jnp.bfloat16),
        acc_up.astype(jnp.bfloat16),
        acc_down.astype(jnp.bfloat16),
    )


def on_device(tokens, cotangent, gate_weight, up_weight, down_weight):
    return stationary(tokens, cotangent, gate_weight, up_weight, down_weight)


def solution(mesh):
    return jax.shard_map(
        on_device,
        mesh=mesh,
        in_specs=(
            P("row", ("depth", "col")),
            P("row", ("depth", "col")),
            P(("depth", "col"), "row"),
            P(("depth", "col"), "row"),
            P("row", ("depth", "col")),
        ),
        out_specs=(
            P("row", ("depth", "col")),
            P(("depth", "col"), "row"),
            P(("depth", "col"), "row"),
            P("row", ("depth", "col")),
        ),
        check_vma=False,
    )
```

profile of v0, /device:TPU:0, one launch (start us, length us, event | category | flops | bytes accessed | tf_op | source)
XLA Modules:
  0.0 501.4 jit_solution(8831859143707906585)
XLA Ops:
  7.2 0.0 slice-start
  7.2 0.0 all-reduce.3.cloned.1.call-start
  7.2 6.8 %all_gather.15 = bf16[192,512]{1,0:T(8,128)(2,1)S(1)} all-gather(bf16[96,512]{1,0:T(8,128)(2,1)} %param.5), channel_id=1, replica_groups=mesh['depth'=4,'row'=2,'col'=4] {'row'}, dimensions={0}, use_global_device_ids=true | all-gather | bytes 294912 | tf_op jit(solution)/shard_map/all_gather | solution.py:29
  14.0 0.0 slice-start.1
  14.0 4.8 fusion.5
  18.9 0.0 slice-done
  18.9 0.0 slice-done.1
  18.9 0.0 copy-start.1
  18.9 1.6 fusion.6
  20.5 0.0 copy-done.1
  20.5 5.3 %all_gather.16 = bf16[192,512]{1,0:T(8,128)(2,1)S(1)} all-gather(bf16[96,512]{1,0:T(8,128)(2,1)S(1)} %copy-done.1), channel_id=1, replica_groups=mesh['depth'=4,'row'=2,'col'=4] {'row'}, dimensions={0}, use_global_device_ids=true | all-gather | bytes 294912 | tf_op jit(solution)/shard_map/all_gather | solution.py:30
  25.8 5.6 %fusion.7 = f32[192,7168]{1,0:T(8,128)S(1)} fusion(bf16[192,512]{1,0:T(8,128)(2,1)S(1)} %all_gather.16, bf16[7168,512]{1,0:T(8,128)(2,1)} %param.9), kind=kOutput, calls=%fused_computation.16 | convolution fusion | flops 1409286144 | bytes 13041664 | tf_op jit(solution)/shard_map/dot_general | solution.py:22
  31.4 6.0 %pad_maximum_fusion = f32[192,21504]{1,0:T(8,128)} fusion(f32[192,7168]{1,0:T(8,128)S(1)} %fusion.7, f32[192,7168]{1,0:T(8,128)S(1)} %fusion.6, f32[192,7168]{1,0:T(8,128)S(1)} %fusion.5), kind=kLoop, calls=%fused_computation | loop fusion | flops 8257536 | bytes 33030144 | tf_op jit(solution)/shard_map/concatenate | solution.py:39
  37.4 0.0 copy-start.2
  37.4 0.0 all-reduce.3.cloned.1.call-update
  37.4 0.0 all-gather.7.cloned.1.call-start
  37.4 0.6 copy-done.2
  38.0 0.6 dynamic-slice
  39.2 292.3 %all-reduce.3.cloned.1.call-done = f32[192,21504]{1,0:T(8,128)} async-done(((f32[192,21504]{1,0:T(8,128)}), f32[192,21504]{1,0:T(8,128)}) %all-reduce.3.cloned.1.call-update) | async-done | bytes 16515088
  331.5 2.7 fusion.3
  334.2 0.0 all-gather.7.cloned.1.call-update
  334.3 0.0 all-gather.9.cloned.1.call-start
  334.3 0.7 all-gather.9.cloned.1.call-update
  335.0 0.0 all-gather.11.cloned.1.call-start
  335.0 0.5 all-gather.11.cloned.1.call-update
  335.6 0.2 reduce-scatter.2.cloned.1.call-start
  335.8 46.3 %all-gather.7.cloned.1.call-done = bf16[16,12,7168]{2,1,0:T(8,128)(2,1)} async-done(((bf16[1,12,7168]{2,1,0:T(8,128)(2,1)}), bf16[16,12,7168]{2,1,0:T(8,128)(2,1)}) %all-gather.7.cloned.1.call-update) | async-done | bytes 2752528 | tf_op jit(solution)/shard_map/all_gather | solution.py:48
  382.1 3.0 reshape.9
  385.2 0.0 copy-start
  385.2 5.2 %fusion = bf16[512,7168]{0,1:T(8,128)(2,1)} fusion(bf16[192,7168]{1,0:T(8,128)(2,1)S(1)} %reshape.9, bf16[192,512]{1,0:T(8,128)(2,1)S(1)} %all_gather.15), kind=kOutput, calls=%fused_computation.4 | convolution fusion | flops 1412956160 | bytes 10289152 | tf_op jit(solution)/shard_map/dot_general | solution.py:16
  390.3 10.0 %copy.13 = bf16[512,7168]{1,0:T(8,128)(2,1)} copy(bf16[512,7168]{0,1:T(8,128)(2,1)} %fusion) | data formatting | bytes 14680064
  400.3 0.0 copy-done
  400.3 30.5 %all-gather.9.cloned.1.call-done = bf16[16,12,7168]{2,1,0:T(8,128)(2,1)} async-done(((bf16[1,12,7168]{2,1,0:T(8,128)(2,1)}), bf16[16,12,7168]{2,1,0:T(8,128)(2,1)}) %all-gather.9.cloned.1.call-update) | async-done | bytes 2752528 | tf_op jit(solution)/shard_map/all_gather | solution.py:49
  430.8 3.0 reshape.11
  433.8 6.5 %fusion.8 = f32[192,512]{1,0:T(8,128)S(1)} fusion(bf16[192,7168]{1,0:T(8,128)(2,1)} %copy-done, bf16[512,7168]{1,0:T(8,128)(2,1)} %param.7), kind=kOutput, calls=%fused_computation.17 | convolution fusion | flops 1409286144 | bytes 10485760 | tf_op jit(solution)/shard_map/dot_general | solution.py:22
  440.3 6.4 %convolution_add_fusion = f32[192,512]{1,0:T(8,128)} fusion(f32[192,512]{1,0:T(8,128)S(1)} %fusion.8, bf16[192,7168]{1,0:T(8,128)(2,1)S(1)} %reshape.11, bf16[512,7168]{1,0:T(8,128)(2,1)} %param.8), kind=kOutput, calls=%fused_computation.6 | convolution fusion | flops 1409384448 | bytes 10878976 | tf_op jit(solution)/shard_map/dot_general | solution.py:22
  446.7 0.0 reduce-scatter.2.cloned.1.call-update
  446.7 5.2 %fusion.1 = bf16[512,7168]{0,1:T(8,128)(2,1)} fusion(bf16[192,7168]{1,0:T(8,128)(2,1)S(1)} %reshape.11, bf16[192,512]{1,0:T(8,128)(2,1)S(1)} %all_gather.15), kind=kOutput, calls=%fused_computation.5 | convolution fusion | flops 1412956160 | bytes 10289152 | tf_op jit(solution)/shard_map/dot_general | solution.py:16
  451.9 10.0 %copy.14 = bf16[512,7168]{1,0:T(8,128)(2,1)} copy(bf16[512,7168]{0,1:T(8,128)(2,1)} %fusion.1) | data formatting | bytes 14680064
  461.9 17.4 %all-gather.11.cloned.1.call-done = bf16[16,12,7168]{2,1,0:T(8,128)(2,1)} async-done(((bf16[1,12,7168]{2,1,0:T(8,128)(2,1)}), bf16[16,12,7168]{2,1,0:T(8,128)(2,1)}) %all-gather.11.cloned.1.call-update) | async-done | bytes 2752528 | tf_op jit(solution)/shard_map/all_gather | solution.py:47
  479.3 3.0 reshape.13
  482.4 5.2 %convolution_convert_fusion = bf16[7168,512]{1,0:T(8,128)(2,1)} fusion(bf16[192,7168]{1,0:T(8,128)(2,1)S(1)} %reshape.13, bf16[192,512]{1,0:T(8,128)(2,1)S(1)} %all_gather.16), kind=kOutput, calls=%fused_computation.1 | convolution fusion | flops 1412956160 | bytes 10289152 | tf_op jit(solution)/shard_map/dot_general | solution.py:16
  487.5 5.8 %reduce-scatter.2.cloned.1.call-done = f32[96,512]{1,0:T(8,128)} async-done(((f32[192,512]{1,0:T(8,128)}), f32[96,512]{1,0:T(8,128)}) %reduce-scatter.2.cloned.1.call-update) | async-done | bytes 196624 | tf_op jit(solution)/shard_map/reduce_scatter | solution.py:56
  493.3 1.6 convert_element_type.29
  (1 shorter events, 0.0 us)
Async XLA Ops:
  7.2 11.7 %slice-start = ((s8[7340032]{0:T(1024)(128)(4,1)}), s8[3145728]{0:T(1024)(128)(4,1)S(1)}, s32[]{:S(2)}) async-start(s8[7340032]{0:T(1024)(128)(4,1)} %bitcast.27), calls=%async_computation.6 | async-start | bytes 6291456
  7.2 324.3 %all-reduce.3.cloned.1.call-start = ((), (), s32[]{:S(2)}) async-start(), calls=%async_computation.5 | async-start | bytes 33030144
  14.0 4.9 slice-start.1
  18.9 1.6 copy-start.1
  37.4 0.7 copy-start.2
  37.4 344.7 %all-gather.7.cloned.1.call-start = ((), (), s32[]{:S(2)}) async-start(), calls=%async_computation.2 | async-start | bytes 3899392 | tf_op jit(solution)/shard_map/all_gather | solution.py:48
  334.3 96.5 %all-gather.9.cloned.1.call-start = ((), (), s32[]{:S(2)}) async-start(), calls=%async_computation.3 | async-start | bytes 3899392 | tf_op jit(solution)/shard_map/all_gather | solution.py:49
  335.0 144.3 %all-gather.11.cloned.1.call-start = ((), (), s32[]{:S(2)}) async-start(), calls=%async_computation.4 | async-start | bytes 3899392 | tf_op jit(solution)/shard_map/all_gather | solution.py:47
  335.6 157.8 %reduce-scatter.2.cloned.1.call-start = ((), (), s32[]{:S(2)}) async-start(), calls=%async_computation.1 | async-start | bytes 589824 | tf_op jit(solution)/shard_map/reduce_scatter | solution.py:56
  385.2 15.2 %copy-start = (bf16[192,7168]{1,0:T(8,128)(2,1)}, bf16[192,7168]{1,0:T(8,128)(2,1)S(1)}, u32[]{:S(2)}) copy-start(bf16[192,7168]{1,0:T(8,128)(2,1)S(1)} %reshape.9) | copy-start | bytes 8257540
Sparse Core Ops, SparseCore 0:
  37.5 293.9 all-reduce.2
  334.4 47.7 all-gather.6
  384.4 46.3 all-gather.8
  432.9 46.3 all-gather.10
  481.4 11.8 reduce-scatter.1
where the time goes:
time: 502 us; the launch traced here: 501 us
  waiting for transfers between devices  393 us (78%)
  matrix products  40.4 us (8%)
  local copies, waits for them, and re-layouts  30.3 us (6%)
  between operations  14.5 us (3%)
  blocking collectives  12.1 us (2%)
  other arithmetic  10.3 us (2%)
    unnamed x6, waiting for transfers between devices  294 us
    all_gather x1, waiting for transfers between devices, stationary(): gate_piece = lax.all_gather(grad_gate, ('depth', 'col'), axis=0, tiled=True)  46.3 us
    all_gather x1, waiting for transfers between devices, stationary(): up_piece = lax.all_gather(grad_up, ('depth', 'col'), axis=0, tiled=True)  30.5 us
    unnamed x16, local copies, waits for them, and re-layouts  30.3 us
    dot_general x3, matrix products, contract_cols(): lax.dot_general(left, right, (((1,), (1,)), ((), ())), preferred_element_...  18.5 us
    all_gather x1, waiting for transfers between devices, stationary(): hidden_piece = lax.all_gather(hidden, ('depth', 'col'), axis=0, tiled=True)  17.4 us
    dot_general x3, matrix products, contract_rows(): lax.dot_general(left, right, (((0,), (0,)), ((), ())), preferred_element_...  15.5 us
  transfers between devices with their start and end apart: 5, of which 5 were waited for; matrix products, arithmetic and copies ran while one was open for 12% of the time, Pallas kernels for 0%

commit v1 on v0

--- a/solution.py
+++ b/solution.py
@@ -44,8 +44,12 @@
     hidden, grad_gate, grad_up = swiglu_back(
         summed[:, :width], summed[:, width : 2 * width], summed[:, 2 * width :]
     )
-    hidden_piece = lax.all_gather(hidden, ("depth", "col"), axis=0, tiled=True)
-    gate_piece = lax.all_gather(grad_gate, ("depth", "col"), axis=0, tiled=True)
+    _turn_patches = lambda xx, load, which_axis: jnp.split(
+        lax.all_gather(jnp.concatenate([xx, load], 1), which_axis, axis=0, tiled=True),
+        [xx.shape[1]],
+        1,
+    )
+    hidden_piece, gate_piece = _turn_patches(hidden, grad_gate, ("depth", "col"))
     up_piece = lax.all_gather(grad_up, ("depth", "col"), axis=0, tiled=True)
     rows_part = rows_all
     cot_part = cot_all

time: 502 us -> 497 us (0.990)
  waiting for transfers between devices: 393 us -> 385 us
    all_gather x2 -> x1, waiting for transfers between devices: 63.7 us -> 45.4 us  [stationary(): lax.all_gather(jnp.concatenate([xx, load], 1), which_axis, axis=0, tiled=...]
    all_gather x1, waiting for transfers between devices: 30.5 us -> 46.9 us  [stationary(): up_piece = lax.all_gather(grad_up, ('depth', 'col'), axis=0, tiled=True)]
    reduce_scatter x1, waiting for transfers between devices: 5.8 us -> 0.01 us  [stationary(): lax.psum_scatter(block, 'row', scatter_dimension=0, tiled=True)]
    unnamed x16 -> x15, local copies, waits for them, and re-layouts: 30.3 us -> 32.5 us
    unnamed x6 -> x5, waiting for transfers between devices: 294 us -> 292 us
  transfers between devices with their start and end apart: 5 -> 4, of which waited for: 5 -> 3; matrix products, arithmetic and copies ran while one was open for 12% -> 10% of each run, Pallas kernels for 0% -> 0%
where the time goes in v1:
time: 497 us; the launch traced here: 496 us
  waiting for transfers between devices  385 us (77%)
  matrix products  41.2 us (8%)
  local copies, waits for them, and re-layouts  32.5 us (7%)
  between operations  14.5 us (3%)
  blocking collectives  12.1 us (2%)
  other arithmetic  10.9 us (2%)
    unnamed x5, waiting for transfers between devices  292 us
    all_gather x1, waiting for transfers between devices, stationary(): up_piece = lax.all_gather(grad_up, ('depth', 'col'), axis=0, tiled=True)  46.9 us
    all_gather x1, waiting for transfers between devices, stationary(): lax.all_gather(jnp.concatenate([xx, load], 1), which_axis, axis=0, tiled=...  45.4 us
    unnamed x15, local copies, waits for them, and re-layouts  32.5 us
    dot_general x3, matrix products, contract_rows(): lax.dot_general(left, right, (((0,), (0,)), ((), ())), preferred_element_...  19.1 us
    dot_general x3, matrix products, contract_cols(): lax.dot_general(left, right, (((1,), (1,)), ((), ())), preferred_element_...  15.5 us
  transfers between devices with their start and end apart: 4, of which 3 were waited for; matrix products, arithmetic and copies ran while one was open for 10% of the time, Pallas kernels for 0%

profile of v1, /device:TPU:0, one launch (start us, length us, event | category | flops | bytes accessed | tf_op | source)
XLA Modules:
  0.0 496.1 jit_solution(1523845829363775441)
XLA Ops:
  7.2 0.0 all-reduce.3.cloned.1.call-start
  7.2 0.0 copy-start
  7.2 6.8 %all_gather.12 = bf16[192,512]{1,0:T(8,128)(2,1)S(1)} all-gather(bf16[96,512]{1,0:T(8,128)(2,1)} %param.5), channel_id=1, replica_groups=mesh['depth'=4,'row'=2,'col'=4] {'row'}, dimensions={0}, use_global_device_ids=true | all-gather | bytes 294912 | tf_op jit(solution)/shard_map/all_gather | solution.py:29
  14.0 0.0 slice-start
  14.0 4.8 fusion.10
  18.9 0.0 copy-done
  18.9 0.0 copy-start.1
  18.9 0.0 slice-start.1
  18.9 1.7 fusion.11
  20.6 0.0 copy-done.1
  20.6 5.3 %all_gather.13 = bf16[192,512]{1,0:T(8,128)(2,1)S(1)} all-gather(bf16[96,512]{1,0:T(8,128)(2,1)S(1)} %copy-done.1), channel_id=1, replica_groups=mesh['depth'=4,'row'=2,'col'=4] {'row'}, dimensions={0}, use_global_device_ids=true | all-gather | bytes 294912 | tf_op jit(solution)/shard_map/all_gather | solution.py:30
  25.9 0.0 slice-done
  25.9 0.0 slice-done.1
  25.9 2.6 fusion.12
  28.5 6.0 %pad_maximum_fusion = f32[192,21504]{1,0:T(8,128)} fusion(f32[192,7168]{1,0:T(8,128)S(1)} %fusion.12, f32[192,7168]{1,0:T(8,128)S(1)} %fusion.11, f32[192,7168]{1,0:T(8,128)S(1)} %fusion.10), kind=kLoop, calls=%fused_computation | loop fusion | flops 8257536 | bytes 33030144 | tf_op jit(solution)/shard_map/concatenate | solution.py:39
  34.5 0.0 copy-start.2
  34.5 0.0 all-reduce.3.cloned.1.call-update
  34.5 0.0 all-gather.7.cloned.1.call-start
  34.5 0.6 copy-done.2
  35.1 0.6 dynamic-slice
  36.4 292.3 %all-reduce.3.cloned.1.call-done = f32[192,21504]{1,0:T(8,128)} async-done(((f32[192,21504]{1,0:T(8,128)}), f32[192,21504]{1,0:T(8,128)}) %all-reduce.3.cloned.1.call-update) | async-done | bytes 16515088
  328.6 2.6 multiply_convert_fusion.2
  331.2 0.0 all-gather.7.cloned.1.call-update
  331.2 0.0 all-gather.5.cloned.1.call-start
  331.3 0.8 maximum_bitcast_fusion
  332.1 0.0 all-gather.5.cloned.1.call-update
  332.1 0.2 reduce-scatter.2.cloned.1.call-start
  332.3 46.9 %all-gather.7.cloned.1.call-done = bf16[16,12,7168]{2,1,0:T(8,128)(2,1)} async-done(((bf16[1,12,7168]{2,1,0:T(8,128)(2,1)}), bf16[16,12,7168]{2,1,0:T(8,128)(2,1)}) %all-gather.7.cloned.1.call-update) | async-done | bytes 2752528 | tf_op jit(solution)/shard_map/all_gather | solution.py:53
  379.2 3.0 reshape.11
  382.3 5.2 %fusion.1 = bf16[512,7168]{0,1:T(8,128)(2,1)} fusion(bf16[192,7168]{1,0:T(8,128)(2,1)S(1)} %reshape.11, bf16[192,512]{1,0:T(8,128)(2,1)S(1)} %all_gather.12), kind=kOutput, calls=%fused_computation.5 | convolution fusion | flops 1412956160 | bytes 10289152 | tf_op jit(solution)/shard_map/dot_general | solution.py:16
  387.4 10.0 %copy.14 = bf16[512,7168]{1,0:T(8,128)(2,1)} copy(bf16[512,7168]{0,1:T(8,128)(2,1)} %fusion.1) | data formatting | bytes 14680064
  397.4 5.7 %fusion.13 = f32[192,512]{1,0:T(8,128)S(1)} fusion(bf16[192,7168]{1,0:T(8,128)(2,1)S(1)} %reshape.11, bf16[512,7168]{1,0:T(8,128)(2,1)} %param.8), kind=kOutput, calls=%fused_computation.20 | convolution fusion | flops 1409286144 | bytes 10485760 | tf_op jit(solution)/shard_map/dot_general | solution.py:22
  403.1 45.4 %all-gather.5.cloned.1.call-done = bf16[16,12,14336]{2,1,0:T(8,128)(2,1)} async-done(((bf16[1,12,14336]{2,1,0:T(8,128)(2,1)}), bf16[16,12,14336]{2,1,0:T(8,128)(2,1)}) %all-gather.5.cloned.1.call-update) | async-done | bytes 5505040 | tf_op jit(solution)/shard_map/all_gather | solution.py:48
  448.5 8.3 %reshape.9 = bf16[192,14336]{1,0:T(8,128)(2,1)} reshape(bf16[16,12,14336]{2,1,0:T(8,128)(2,1)} %all-gather.5.cloned.1.call-done) | data formatting | bytes 11010048
  456.8 7.2 %fusion.6 = f32[192,512]{1,0:T(8,128)} fusion(f32[192,512]{1,0:T(8,128)S(1)} %fusion.13, bf16[512,7168]{1,0:T(8,128)(2,1)} %param.7, bf16[192,14336]{1,0:T(8,128)(2,1)} %reshape.9), kind=kOutput, calls=%fused_computation.10 | convolution fusion | flops 1409384448 | bytes 10878976 | tf_op jit(solution)/shard_map/dot_general | solution.py:22
  464.0 0.0 reduce-scatter.2.cloned.1.call-update
  464.1 7.0 %fusion = bf16[512,7168]{0,1:T(8,128)(2,1)} fusion(bf16[192,512]{1,0:T(8,128)(2,1)S(1)} %all_gather.12, bf16[192,14336]{1,0:T(8,128)(2,1)} %reshape.9), kind=kOutput, calls=%fused_computation.4 | convolution fusion | flops 1412956160 | bytes 10289152 | tf_op jit(solution)/shard_map/dot_general | solution.py:16
  471.1 9.9 %copy.13 = bf16[512,7168]{1,0:T(8,128)(2,1)} copy(bf16[512,7168]{0,1:T(8,128)(2,1)} %fusion) | data formatting | bytes 14680064
  481.0 7.0 %convolution_convert_fusion = bf16[7168,512]{1,0:T(8,128)(2,1)} fusion(bf16[192,512]{1,0:T(8,128)(2,1)S(1)} %all_gather.13, bf16[192,14336]{1,0:T(8,128)(2,1)} %reshape.9), kind=kOutput, calls=%fused_computation.1 | convolution fusion | flops 1412956160 | bytes 10289152 | tf_op jit(solution)/shard_map/dot_general | solution.py:16
  488.0 0.0 reduce-scatter.2.cloned.1.call-done
  488.0 1.6 convert_element_type.30
  (1 shorter events, 0.0 us)
Async XLA Ops:
  7.2 321.4 %all-reduce.3.cloned.1.call-start = ((), (), s32[]{:S(2)}) async-start(), calls=%async_computation.4 | async-start | bytes 33030144
  7.2 11.6 %copy-start = (bf16[512,7168]{1,0:T(8,128)(2,1)S(1)}, bf16[512,7168]{1,0:T(8,128)(2,1)}, u32[]{:S(2)}) copy-start(bf16[512,7168]{1,0:T(8,128)(2,1)} %param.8) | copy-start | bytes 22020100
  14.0 11.9 %slice-start = ((s8[7340032]{0:T(1024)(128)(4,1)}), s8[4194304]{0:T(1024)(128)(4,1)S(1)}, s32[]{:S(2)}) async-start(s8[7340032]{0:T(1024)(128)(4,1)} %bitcast.22), calls=%async_computation.5 | async-start | bytes 8388608
  18.9 1.8 copy-start.1
  18.9 7.1 %slice-start.1 = ((s8[7340032]{0:T(1024)(128)(4,1)}), s8[3145728]{0:T(1024)(128)(4,1)S(1)}, s32[]{:S(2)}) async-start(s8[7340032]{0:T(1024)(128)(4,1)} %bitcast.22), calls=%async_computation.6 | async-start | bytes 6291456
  34.5 0.7 copy-start.2
  34.5 344.7 %all-gather.7.cloned.1.call-start = ((), (), s32[]{:S(2)}) async-start(), calls=%async_computation.3 | async-start | bytes 3899392 | tf_op jit(solution)/shard_map/all_gather | solution.py:53
  331.2 117.3 %all-gather.5.cloned.1.call-start = ((), (), s32[]{:S(2)}) async-start(), calls=%async_computation.2 | async-start | bytes 7798784 | tf_op jit(solution)/shard_map/all_gather | solution.py:48
  332.1 155.9 %reduce-scatter.2.cloned.1.call-start = ((), (), s32[]{:S(2)}) async-start(), calls=%async_computation.1 | async-start | bytes 589824 | tf_op jit(solution)/shard_map/reduce_scatter | solution.py:60
Sparse Core Ops, SparseCore 0:
  34.6 293.9 all-reduce.2
  331.5 47.7 all-gather.6
  382.1 66.3 all-gather.4
  464.2 11.9 reduce-scatter.1
